TPU v7x, 32 devices: a whole 2x2x4 slice. The times are simulated.
32 devices in a mesh: row: 8 (over z, x), col: 4 (over y, core).
Axes of the slice: x: 2, y: 2, z: 4, core: 2. Of those that a mesh axis runs over, the one named last changes fastest.
Arguments:
- queries: bfloat16 [8192, 2048], P(('row', 'col')), may hold values from -200 to 200
- keys: bfloat16 [8192, 512], P(('row', 'col')), may hold values from -6 to 6
- values: bfloat16 [8192, 512], P(('row', 'col')), may hold values from -6 to 6
- mid_key_weight: bfloat16 [1024, 128], replicated, may hold values from -0.1875 to 0.1875
- mid_value_weight: bfloat16 [1024, 128], replicated, may hold values from -0.1875 to 0.1875
- far_key_weight: bfloat16 [2048, 128], replicated, may hold values from -0.125 to 0.125
- far_value_weight: bfloat16 [2048, 128], replicated, may hold values from -0.125 to 0.125
Outputs:
- attended: bfloat16 [8192, 2048], P(('row', 'col'))
All inputs are finite; a program needn't handle non-finite values.
Results may differ from a plain program's by a relative error of at most 0.012.
Values may be sent and summed in bfloat16 or wider, within the bound.
A program may use at most 128 MiB of HBM per device.

v0:
```python
import jax
import jax.numpy as jnp
from jax import lax
from jax.sharding import PartitionSpec as P

HQ = 16
HK = 4
DH = 128
BLOCK = 512
MID = 8
FAR = 16


NEG_FILL = -1e30


def from_behind(block, axis, distance):
    devices = range(lax.axis_size(axis))
    route = [(i - distance, i) for i in devices if i - distance in devices]
    return lax.ppermute(block, axis, route)


def squeeze_groups(source, weight, squeeze):
    group_count = source.shape[0] // squeeze
    grouped = (
        source.reshape(group_count, squeeze, HK, DH)
        .transpose(0, 2, 1, 3)
        .reshape(group_count, HK, squeeze * DH)
    )
    merged = jnp.einsum("nhr,rd->nhd", grouped, weight, preferred_element_type=jnp.float32)
    return merged.astype(jnp.bfloat16).reshape(group_count, HK * DH)


def attend(queries, keys, values, visible):
    group_size = HQ // HK
    query_rows = queries.shape[0]
    query4 = queries.reshape(query_rows, HK, group_size, DH)
    key_heads = keys.reshape(keys.shape[0], HK, DH)
    value_heads = values.reshape(values.shape[0], HK, DH)
    scores = jnp.einsum(
        "thgd,shd->hgts", query4, key_heads, preferred_element_type=jnp.float32
    ) * DH ** (-0.5)
    top_score = jnp.max(jnp.where(visible, scores, NEG_FILL), axis=-1, keepdims=True)
    weights = jnp.exp(jnp.where(visible, scores - top_score, NEG_FILL))
    weight_sum = jnp.sum(weights, axis=-1)
    mixed_out = jnp.einsum(
        "hgts,shd->thgd",
        weights.astype(jnp.bfloat16),
        value_heads,
        preferred_element_type=jnp.float32,
    )
    weight_sum = jnp.transpose(weight_sum, (2, 0, 1))[..., None]
    return (mixed_out / jnp.maximum(weight_sum, 1.0)).reshape(query_rows, HQ * DH)


def body(queries, keys, values, mid_key_weight, mid_value_weight, far_key_weight, far_value_weight):
    tok_rows = queries.shape[0]
    columns = lax.axis_size("col")
    device_pos = lax.axis_index(("row", "col"))
    grid_row = device_pos // columns
    first_pos = device_pos * tok_rows
    query_pos = first_pos + jnp.arange(tok_rows, dtype=jnp.int32)
    near_pair = jnp.stack((keys, values))
    window = [near_pair]
    for offset in (1, 2, 3):
        window.insert(0, from_behind(near_pair, ("row", "col"), offset))
    near_all = jnp.concatenate(window, axis=1)
    key_pos = first_pos - 3 * tok_rows + jnp.arange(4 * tok_rows, dtype=jnp.int32)
    near_seen = (
        (key_pos[None, :] <= query_pos[:, None])
        & (key_pos[None, :] >= 0)
        & (key_pos[None, :] // BLOCK >= query_pos[:, None] // BLOCK - 1)
    )
    near_out = attend(queries, near_all[0], near_all[1], near_seen)
    mid_pair = jnp.stack(
        (squeeze_groups(keys, mid_key_weight, MID), squeeze_groups(values, mid_value_weight, MID))
    )
    far_pair = jnp.stack(
        (squeeze_groups(keys, far_key_weight, FAR), squeeze_groups(values, far_value_weight, FAR))
    )
    row_mid, row_far = (
        lax.all_gather(mid_pair, "col", axis=1, tiled=True),
        lax.all_gather(far_pair, "col", axis=1, tiled=True),
    )
    all_far = lax.all_gather(row_far, "row", axis=1, tiled=True)
    mid_count = row_mid.shape[1]
    mid_end = (
        grid_row * (columns * tok_rows) + MID * jnp.arange(mid_count, dtype=jnp.int32) + MID - 1
    )
    mid_out = attend(queries, row_mid[0], row_mid[1], mid_end[None, :] <= query_pos[:, None])
    far_count = all_far.shape[1]
    far_row = jnp.arange(far_count, dtype=jnp.int32) // (columns * tok_rows // FAR)
    far_mask = far_row < grid_row
    block_rows = min(64, tok_rows)
    query_blocks = queries.reshape(tok_rows // block_rows, block_rows, queries.shape[1])

    def far_block(query_block):
        seen = jnp.broadcast_to(far_mask[None, :], (block_rows, far_count))
        return attend(query_block, all_far[0], all_far[1], seen)

    far_out = lax.map(far_block, query_blocks).reshape(tok_rows, queries.shape[1])
    return (near_out + mid_out + far_out).astype(jnp.bfloat16)


def solution(mesh):
    return jax.shard_map(
        body,
        mesh=mesh,
        in_specs=(
            P(("row", "col"), None),
            P(("row", "col"), None),
            P(("row", "col"), None),
            P(),
            P(),
            P(),
            P(),
        ),
        out_specs=P(("row", "col"), None),
        check_vma=False,
    )
```

profile of v0, /device:TPU:0, one launch (start us, length us, event | category | flops | bytes accessed | tf_op | source)
XLA Modules:
  0.0 125.0 jit_solution(5251850625386696170)
XLA Ops:
  6.5 1.2 copy.22
  7.7 1.1 copy.23
  8.9 5.3 %collective-permute-start = (bf16[2,256,512]{1,2,0:T(8,128)(2,1)S(1)}, bf16[2,256,512]{1,2,0:T(8,128)(2,1)}, u32[]{:S(2)}, u32[]{:S(2)}) collective-permute-start(bf16[2,256,512]{1,2,0:T(8,128)(2,1)S(1)} %pad_maximum_fusion), channel_id=1, source_target_pairs={{0,3},{1,4},{2,5},{3,6},{4,7},{5,8},{6,9},{7,10},{8,11},{9,12},{10... | collective-permute-start | bytes 1572872 | tf_op jit(solution)/shard_map/ppermute | solution.py:20
  14.2 4.1 %collective-permute-start.1 = (bf16[2,256,512]{1,2,0:T(8,128)(2,1)S(1)}, bf16[2,256,512]{1,2,0:T(8,128)(2,1)}, u32[]{:S(2)}, u32[]{:S(2)}) collective-permute-start(bf16[2,256,512]{1,2,0:T(8,128)(2,1)S(1)} %pad_maximum_fusion), channel_id=1, source_target_pairs={{0,2},{1,3},{2,4},{3,5},{4,6},{5,7},{6,8},{7,9},{8,10},{9,11},{10,... | collective-permute-start | bytes 1572872 | tf_op jit(solution)/shard_map/ppermute | solution.py:20
  18.3 2.4 %collective-permute-start.2 = (bf16[2,256,512]{1,2,0:T(8,128)(2,1)S(1)}, bf16[2,256,512]{1,2,0:T(8,128)(2,1)}, u32[]{:S(2)}, u32[]{:S(2)}) collective-permute-start(bf16[2,256,512]{1,2,0:T(8,128)(2,1)S(1)} %pad_maximum_fusion), channel_id=1, source_target_pairs={{0,1},{1,2},{2,3},{3,4},{4,5},{5,6},{6,7},{7,8},{8,9},{9,10},{10,1... | collective-permute-start | bytes 1572872 | tf_op jit(solution)/shard_map/ppermute | solution.py:20
  21.8 12.7 %all_gather.10 = bf16[2,64,512]{2,1,0:T(8,128)(2,1)} all-gather(bf16[2,16,512]{2,1,0:T(8,128)(2,1)S(1)} %pad_maximum_fusion.2), channel_id=1, replica_groups=mesh['row'=8,'col'=4] {'col'}, dimensions={1}, use_global_device_ids=true | all-gather | bytes 163840 | tf_op jit(solution)/shard_map/all_gather | solution.py:83
  35.3 11.0 %all_gather.9 = bf16[2,128,512]{2,1,0:T(8,128)(2,1)S(1)} all-gather(bf16[2,32,512]{2,1,0:T(8,128)(2,1)S(1)} %pad_maximum_fusion.1), channel_id=1, replica_groups=mesh['row'=8,'col'=4] {'col'}, dimensions={1}, use_global_device_ids=true | all-gather | bytes 327680 | tf_op jit(solution)/shard_map/all_gather | solution.py:82
  46.4 1.8 %reshape.143 = bf16[256,4,4,128]{3,2,1,0:T(4,128)(2,1)S(1)} reshape(bf16[256,2048]{1,0:T(8,128)(2,1)} %param.9) | data formatting | bytes 2097152 | tf_op jit(solution)/shard_map/reshape | solution.py:37
  50.3 1.5 %compare_and_fusion = pred[256,1024]{0,1:T(8,128)(4,1)} fusion(s32[256]{0:T(256)S(1)} %get-tuple-element.69, s32[256]{0:T(256)S(1)} %get-tuple-element.70, s32[1024]{0:T(1024)S(1)} %get-tuple-element.71, s32[1024]{0:T(1024)S(1)} %get-tuple-element.72, pred[1024]{0:T(1024)(128)(4,1)S(1)} %fusion.68), kind=kLoop, calls=%fused_computation.67 | loop fusion | flops 1048576 | bytes 273408 | tf_op jit(solution)/shard_map/and | solution.py:70
  51.8 4.5 %fusion.46 = f32[4,128,4,256]{3,1,2,0:T(8,128)} fusion(bf16[128,4,128,1]{0,2,3,1:T(8,128)(2,1)S(1)} %bitcast.188, f32[4,128,256,4]{2,1,3,0:T(8,128)} %copy-done.3, pred[256,128]{0,1:T(8,128)(4,1)S(1)} %broadcast_compare_fusion), kind=kOutput, calls=%fused_computation.62 | convolution fusion | flops 137367680 | bytes 4358144 | tf_op jit(solution)/shard_map/hgts,shd->thgd/dot_general | solution.py:46
  56.4 1.5 %maximum_maximum_fusion = bf16[2,1024,512]{1,2,0:T(8,128)(2,1)S(1)} fusion(bf16[1,256,512]{1,2,0:T(8,128)(2,1)S(1)} %bitcast.181, bf16[1,256,512]{1,2,0:T(8,128)(2,1)S(1)} %bitcast.179, bf16[2,256,512]{1,2,0:T(8,128)(2,1)} %collective-permute-done.2, bf16[2,256,512]{1,2,0:T(8,128)(2,1)} %collective-permute-done.1, bf16[2,256,512]{1,2,0:T(8,128)(2,1)} %collective-permute-done), kind=kLoop, calls=%fused_computation.45 | loop fusion | flops 10485760 | bytes 4194304 | tf_op jit(solution)/shard_map/concatenate | solution.py:67
  57.9 1.1 fusion.82
  59.1 9.8 %fusion.85 = (f32[4,4,256]{2,1,0:T(4,128)S(1)}, bf16[4,4,256,1024]{2,3,1,0:T(8,128)(2,1)}) fusion(pred[256,1024]{0,1:T(8,128)(4,1)S(1)} %copy-done.7, bf16[1024,4,128,1]{0,2,3,1:T(8,128)(2,1)S(1)} %bitcast.186, bf16[256,4,4,128]{3,2,1,0:T(4,128)(2,1)S(1)} %reshape.143), kind=kOutput, calls=%fused_computation.114 | convolution fusion | flops 2176844800 | bytes 10764288 | tf_op jit(solution)/shard_map/sub | solution.py:44
  68.9 5.6 %fusion.37 = f32[256,4,4,128]{0,3,2,1:T(8,128)S(1)} fusion(f32[4,128,4,256]{3,1,2,0:T(8,128)} %fusion.46, bf16[1024,4,128,1]{0,2,3,1:T(8,128)(2,1)} %bitcast.185, bf16[4,4,256,1024]{2,3,1,0:T(8,128)(2,1)} %get-tuple-element.68, f32[256,4,4]{0,2,1:T(4,128)S(1)} %maximum_bitcast_fusion.1, f32[256,4,4]{0,2,1:T(4,128)S(1)} %maximum_bitcast_fusion.2), kind=kOutput, calls=%fused_computation.49 | convolution fusion | flops 1075314688 | bytes 13664256 | tf_op jit(solution)/shard_map/hgts,shd->thgd/dot_general | solution.py:46
  74.5 1.9 %copy.41 = f32[256,2048]{1,0:T(8,128)} copy(f32[256,2048]{0,1:T(8,128)S(1)} %bitcast.182) | data formatting | bytes 4194304 | tf_op jit(solution)/shard_map/add | solution.py:102
  76.4 4.8 %all-gather.2.cloned.1.call-done = bf16[2,512,512]{2,1,0:T(8,128)(2,1)} async-done(((bf16[2,64,512]{2,1,0:T(8,128)(2,1)}), bf16[2,512,512]{2,1,0:T(8,128)(2,1)}) %all-gather.2.cloned.1.call-update) | async-done | bytes 1048592 | tf_op jit(solution)/shard_map/all_gather | solution.py:85
  81.2 2.3 %copy.40 = bf16[2,512,512]{1,2,0:T(8,128)(2,1)} copy(bf16[2,512,512]{2,1,0:T(8,128)(2,1)} %all-gather.2.cloned.1.call-done) | data formatting | bytes 2097152
  83.5 31.2 %while.11 = (s32[]{:T(128)}, f32[4,64,2048]{2,1,0:T(8,128)}, bf16[4,64,2048]{2,1,0:T(8,128)(2,1)}, bf16[2,512,512]{1,2,0:T(8,128)(2,1)}, s32[]{:T(128)}, /*index=5*/s32[]{:T(128)}) while((s32[]{:T(128)}, f32[4,64,2048]{2,1,0:T(8,128)}, bf16[4,64,2048]{2,1,0:T(8,128)(2,1)}, bf16[2,512,512]{1,2,0:T(8,128)(2,1)}, s32[]{:T(128)}, ...), condition=%wide.region_7.8_spmd.clone, body=%wide.region_4.7_spmd.clone.sunk | while | flops 274865664 | bytes 14436429 | solution.py:101
  83.5 1.0 constant_dynamic-slice_fusion.2
  84.6 2.1 %fusion.113 = (bf16[1,512,512]{1,2,0:T(8,128)(2,1)S(1)}, bf16[1,512,512]{1,2,0:T(8,128)(2,1)}) fusion(bf16[2,512,512]{1,2,0:T(8,128)(2,1)} %get-tuple-element.125), kind=kLoop, calls=%fused_computation.109.clone.1 | loop fusion | bytes 2097152 | tf_op jit(solution)/shard_map/while/body/eval_jaxpr/slice | solution.py:99
  87.9 1.9 %fusion.117 = f32[64,4,4,128]{3,0,2,1:T(8,128)S(1)} fusion(bf16[512,4,128,1]{0,2,3,1:T(8,128)(2,1)} %bitcast.175, f32[64,4,4]{0,2,1:T(4,128)S(1)} %maximum_bitcast_fusion.4, f32[4,64,4,512]{3,1,2,0:T(8,128)S(1)} %fusion.114, pred[512]{0:T(512)(128)(4,1)S(1)} %fusion.115), kind=kOutput, calls=%fused_computation.9.clone.1 | convolution fusion | flops 137496064 | bytes 3150336 | tf_op jit(solution)/shard_map/while/body/eval_jaxpr/hgts,shd->thgd/dot_general | solution.py:46
  91.3 1.0 constant_dynamic-slice_fusion.2
  92.4 2.1 %fusion.113 = (bf16[1,512,512]{1,2,0:T(8,128)(2,1)S(1)}, bf16[1,512,512]{1,2,0:T(8,128)(2,1)}) fusion(bf16[2,512,512]{1,2,0:T(8,128)(2,1)} %get-tuple-element.125), kind=kLoop, calls=%fused_computation.109.clone.1 | loop fusion | bytes 2097152 | tf_op jit(solution)/shard_map/while/body/eval_jaxpr/slice | solution.py:99
  95.7 1.9 %fusion.117 = f32[64,4,4,128]{3,0,2,1:T(8,128)S(1)} fusion(bf16[512,4,128,1]{0,2,3,1:T(8,128)(2,1)} %bitcast.175, f32[64,4,4]{0,2,1:T(4,128)S(1)} %maximum_bitcast_fusion.4, f32[4,64,4,512]{3,1,2,0:T(8,128)S(1)} %fusion.114, pred[512]{0:T(512)(128)(4,1)S(1)} %fusion.115), kind=kOutput, calls=%fused_computation.9.clone.1 | convolution fusion | flops 137496064 | bytes 3150336 | tf_op jit(solution)/shard_map/while/body/eval_jaxpr/hgts,shd->thgd/dot_general | solution.py:46
  98.2 0.9 constant_dynamic-update-slice_fusion.2
  99.1 1.0 constant_dynamic-slice_fusion.2
  100.3 2.1 %fusion.113 = (bf16[1,512,512]{1,2,0:T(8,128)(2,1)S(1)}, bf16[1,512,512]{1,2,0:T(8,128)(2,1)}) fusion(bf16[2,512,512]{1,2,0:T(8,128)(2,1)} %get-tuple-element.125), kind=kLoop, calls=%fused_computation.109.clone.1 | loop fusion | bytes 2097152 | tf_op jit(solution)/shard_map/while/body/eval_jaxpr/slice | solution.py:99
  103.6 1.9 %fusion.117 = f32[64,4,4,128]{3,0,2,1:T(8,128)S(1)} fusion(bf16[512,4,128,1]{0,2,3,1:T(8,128)(2,1)} %bitcast.175, f32[64,4,4]{0,2,1:T(4,128)S(1)} %maximum_bitcast_fusion.4, f32[4,64,4,512]{3,1,2,0:T(8,128)S(1)} %fusion.114, pred[512]{0:T(512)(128)(4,1)S(1)} %fusion.115), kind=kOutput, calls=%fused_computation.9.clone.1 | convolution fusion | flops 137496064 | bytes 3150336 | tf_op jit(solution)/shard_map/while/body/eval_jaxpr/hgts,shd->thgd/dot_general | solution.py:46
  106.9 1.0 constant_dynamic-slice_fusion.2
  108.0 2.1 %fusion.113 = (bf16[1,512,512]{1,2,0:T(8,128)(2,1)S(1)}, bf16[1,512,512]{1,2,0:T(8,128)(2,1)}) fusion(bf16[2,512,512]{1,2,0:T(8,128)(2,1)} %get-tuple-element.125), kind=kLoop, calls=%fused_computation.109.clone.1 | loop fusion | bytes 2097152 | tf_op jit(solution)/shard_map/while/body/eval_jaxpr/slice | solution.py:99
  111.3 1.9 %fusion.117 = f32[64,4,4,128]{3,0,2,1:T(8,128)S(1)} fusion(bf16[512,4,128,1]{0,2,3,1:T(8,128)(2,1)} %bitcast.175, f32[64,4,4]{0,2,1:T(4,128)S(1)} %maximum_bitcast_fusion.4, f32[4,64,4,512]{3,1,2,0:T(8,128)S(1)} %fusion.114, pred[512]{0:T(512)(128)(4,1)S(1)} %fusion.115), kind=kOutput, calls=%fused_computation.9.clone.1 | convolution fusion | flops 137496064 | bytes 3150336 | tf_op jit(solution)/shard_map/while/body/eval_jaxpr/hgts,shd->thgd/dot_general | solution.py:46
  114.7 3.5 %fusion.36 = bf16[256,2048]{1,0:T(8,128)(2,1)} fusion(f32[256,2048]{1,0:T(8,128)} %copy.41, f32[4,64,2048]{2,1,0:T(8,128)} %get-tuple-element.32), kind=kLoop, calls=%fused_computation.47 | loop fusion | flops 1048576 | bytes 5242880 | tf_op jit(solution)/shard_map/convert_element_type | solution.py:102
  (88 shorter events, 14.3 us)
Async XLA Ops:
  6.5 14.5 %copy-start = (bf16[2048,128]{1,0:T(8,128)(2,1)S(1)}, bf16[2048,128]{1,0:T(8,128)(2,1)}, u32[]{:S(2)}) copy-start(bf16[2048,128]{1,0:T(8,128)(2,1)} %param.14) | copy-start | bytes 1572868
  6.5 14.1 %copy-start.1 = (bf16[256,512]{1,0:T(8,128)(2,1)S(1)}, bf16[256,512]{1,0:T(8,128)(2,1)}, u32[]{:S(2)}) copy-start(bf16[256,512]{1,0:T(8,128)(2,1)} %param.10) | copy-start | bytes 786436
  6.5 14.2 %copy-start.2 = (bf16[256,512]{1,0:T(8,128)(2,1)S(1)}, bf16[256,512]{1,0:T(8,128)(2,1)}, u32[]{:S(2)}) copy-start(bf16[256,512]{1,0:T(8,128)(2,1)} %param.11) | copy-start | bytes 786436
  6.5 74.6 %all-gather.2.cloned.1.call-start = ((), (), s32[]{:S(2)}) async-start(), calls=%async_computation | async-start | bytes 1179648 | tf_op jit(solution)/shard_map/all_gather | solution.py:85
  8.9 12.6 %copy-start.4 = (bf16[2048,128]{1,0:T(8,128)(2,1)S(1)}, bf16[2048,128]{1,0:T(8,128)(2,1)}, u32[]{:S(2)}) copy-start(bf16[2048,128]{1,0:T(8,128)(2,1)} %param.15) | copy-start | bytes 1572868
  8.9 47.5 %collective-permute-start = (bf16[2,256,512]{1,2,0:T(8,128)(2,1)S(1)}, bf16[2,256,512]{1,2,0:T(8,128)(2,1)}, u32[]{:S(2)}, u32[]{:S(2)}) collective-permute-start(bf16[2,256,512]{1,2,0:T(8,128)(2,1)S(1)} %pad_maximum_fusion), channel_id=1, source_target_pairs={{0,3},{1,4},{2,5},{3,6},{4,7},{5,8},{6,9},{7,10},{8,11},{9,12},{10... | collective-permute-start | bytes 1572872 | tf_op jit(solution)/shard_map/ppermute | solution.py:20
  14.2 42.2 %collective-permute-start.1 = (bf16[2,256,512]{1,2,0:T(8,128)(2,1)S(1)}, bf16[2,256,512]{1,2,0:T(8,128)(2,1)}, u32[]{:S(2)}, u32[]{:S(2)}) collective-permute-start(bf16[2,256,512]{1,2,0:T(8,128)(2,1)S(1)} %pad_maximum_fusion), channel_id=1, source_target_pairs={{0,2},{1,3},{2,4},{3,5},{4,6},{5,7},{6,8},{7,9},{8,10},{9,11},{10,... | collective-permute-start | bytes 1572872 | tf_op jit(solution)/shard_map/ppermute | solution.py:20
  18.3 38.1 %collective-permute-start.2 = (bf16[2,256,512]{1,2,0:T(8,128)(2,1)S(1)}, bf16[2,256,512]{1,2,0:T(8,128)(2,1)}, u32[]{:S(2)}, u32[]{:S(2)}) collective-permute-start(bf16[2,256,512]{1,2,0:T(8,128)(2,1)S(1)} %pad_maximum_fusion), channel_id=1, source_target_pairs={{0,1},{1,2},{2,3},{3,4},{4,5},{5,6},{6,7},{7,8},{8,9},{9,10},{10,1... | collective-permute-start | bytes 1572872 | tf_op jit(solution)/shard_map/ppermute | solution.py:20
  21.3 13.3 %copy-start.5 = (bf16[1024,128]{1,0:T(8,128)(2,1)S(1)}, bf16[1024,128]{1,0:T(8,128)(2,1)}, u32[]{:S(2)}) copy-start(bf16[1024,128]{1,0:T(8,128)(2,1)} %param.12) | copy-start | bytes 786436
  21.5 13.5 %copy-start.6 = (bf16[1024,128]{1,0:T(8,128)(2,1)S(1)}, bf16[1024,128]{1,0:T(8,128)(2,1)}, u32[]{:S(2)}) copy-start(bf16[1024,128]{1,0:T(8,128)(2,1)} %param.13) | copy-start | bytes 786436
  48.8 1.4 %copy-start.3 = (f32[4,128,256,4]{2,1,3,0:T(8,128)}, f32[4,128,256,4]{2,1,3,0:T(8,128)S(1)}, u32[]{:S(2)}) copy-start(f32[4,128,256,4]{2,1,3,0:T(8,128)S(1)} %fusion.54) | copy-start | bytes 6291460
  57.9 1.2 copy-start.7
Sparse Core Ops, SparseCore 0:
  34.6 46.5 all-gather.1
where the time goes:
time: 126 us; the launch traced here: 125 us
  matrix products  30.6 us (24%)
  local copies, waits for them, and re-layouts  29.4 us (23%)
  blocking collectives  23.7 us (19%)
  between operations  13.8 us (11%)
  starting transfers between devices  11.8 us (9%)
  other arithmetic  10.7 us (8%)
  waiting for transfers between devices  4.8 us (4%)
    dot_general x6, matrix products, attend(): jnp.einsum('hgts,shd->thgd', weights.astype(jnp.bfloat16), value_heads, p...  17.8 us
    all_gather x1, blocking collectives, body(): lax.all_gather(far_pair, 'col', axis=1, tiled=True)  12.7 us
    ppermute x3, starting transfers between devices, from_behind(): return lax.ppermute(block, axis, route)  11.8 us
    all_gather x1, blocking collectives, body(): lax.all_gather(mid_pair, 'col', axis=1, tiled=True)  11 us
    sub x1, matrix products, attend(): weights = jnp.exp(jnp.where(visible, scores - top_score, NEG_FILL))  9.82 us
    slice x4, local copies, waits for them, and re-layouts, far_block(): return attend(query_block, all_far[0], all_far[1], seen)  8.27 us
    unnamed x19, local copies, waits for them, and re-layouts  5.15 us
    all_gather x1, waiting for transfers between devices, body(): all_far = lax.all_gather(row_far, 'row', axis=1, tiled=True)  4.78 us
  transfers between devices with their start and end apart: 4, of which 1 were waited for; matrix products, arithmetic and copies ran while one was open for 25% of the time, Pallas kernels for 0%

commit v1 on v0

v1 whole, which is shorter than its diff:
```python
import functools
import math

import jax
import jax.numpy as jnp
from jax import lax
from jax.experimental import pallas as pl
from jax.experimental.pallas import tpu as pltpu
from jax.sharding import PartitionSpec as P

HQ = 16
HK = 4
DH = 128
BLOCK = 512
MID = 8
FAR = 16
GROUP = HQ // HK
KV = HK * DH
NEG_FILL = -1e30
EXP_SCALE = DH ** (-0.5) * math.log2(math.e)
FAR_CHUNK = 512
MESH = pl.DeviceIdType.MESH
FROM_PARTNER, FROM_BEHIND, RELAYED = 0, 1, 2


def score(q, k):
    return lax.dot_general(q, k, (((1,), (1,)), ((), ())), preferred_element_type=jnp.float32)


def weigh(p, v):
    both = jnp.concatenate([v, jnp.ones_like(v)], axis=1)
    return jnp.dot(p.astype(jnp.bfloat16), both, preferred_element_type=jnp.float32)


def powers(s, top):
    return jnp.exp2((s - top) * EXP_SCALE)


def normalised(acc):
    return acc[:, :DH] / jnp.maximum(acc[:, DH:], 1.0)


def kernel(
    rows, cols,
    q_ref, k_ref, v_ref, wmk_ref, wmv_ref, wfk_ref, wfv_ref, out_ref,
    wide, mid_buf, far_own, far_buf, near, top_ref, acc_ref, rest_ref,
    near_send, near_recv, mid_send, mid_recv,
    f1_send, f1_recv, f2_send, f2_recv, f3_send, f3_recv,
):
    tok = q_ref.shape[0]
    mids, fars = tok // MID, tok // FAR
    total = rows * cols
    pairs = cols // 2
    row, col = lax.axis_index("row"), lax.axis_index("col")
    pos = row * cols + col
    side = lax.rem(col, 2)
    pair = col // 2
    other = col + 1 - 2 * side
    partner = (row, other)

    def at(linear):
        return (linear // cols, lax.rem(linear, cols))

    mid_buf[...] = jnp.zeros_like(mid_buf)

    def clear(c, _):
        far_buf[c] = jnp.zeros(far_buf.shape[1:], far_buf.dtype)
        return 0

    lax.fori_loop(0, cols, clear, 0)

    barrier = pltpu.get_barrier_semaphore()

    def greet(device):
        pl.semaphore_signal(barrier, inc=1, device_id=device, device_id_type=MESH)

    def greet_col(i, _):
        greet((row, lax.rem(col + i, cols)))
        return 0

    def greet_row(i, _):
        greet((lax.rem(row + i, rows), col))
        return 0

    lax.fori_loop(1, cols, greet_col, 0)
    lax.fori_loop(1, rows, greet_row, 0)
    greet(at(lax.rem(pos + 2, total)))
    greet(at(lax.rem(pos + total - 2, total)))

    mid_rows = pl.ds(pl.multiple_of(col * mids, mids), mids)
    for s, (src, wm, wf) in enumerate(((k_ref, wmk_ref, wfk_ref), (v_ref, wmv_ref, wfv_ref))):
        for h in range(HK):
            wide[s * HK + h] = src[:, h * DH:(h + 1) * DH].astype(jnp.float32)
        for squeeze, count, weight in ((FAR, fars, wf), (MID, mids, wm)):
            grouped = jnp.concatenate(
                [
                    jnp.concatenate(
                        [wide[s * HK + h, pl.ds(i, count, stride=squeeze), :] for h in range(HK)],
                        axis=0,
                    ).astype(jnp.bfloat16)
                    for i in range(squeeze)
                ],
                axis=1,
            )
            merged = jnp.dot(grouped, weight[...], preferred_element_type=jnp.float32)
            merged = merged.astype(jnp.bfloat16)
            for h in range(HK):
                lanes = slice(s * KV + h * DH, s * KV + (h + 1) * DH)
                piece = merged[h * count:(h + 1) * count]
                if squeeze == FAR:
                    far_own[:, lanes] = piece
                else:
                    mid_buf[mid_rows, lanes] = piece

    pl.semaphore_wait(barrier, cols + rows)

    def remote(src, dst, send, recv, device):
        return pltpu.make_async_remote_copy(
            src_ref=src, dst_ref=dst, send_sem=send, recv_sem=recv,
            device_id=device, device_id_type=MESH,
        )

    def far_slot(c, r):
        return far_buf.at[c, pl.ds(pl.multiple_of(r * fars, fars), fars), :]

    def far1(r_to, r_from):
        return remote(far_own, far_slot(col, r_from), f1_send.at[r_to], f1_recv.at[r_from], (r_to, col))

    def far2(r, p_to, p_from):
        return remote(
            far_slot(2 * p_from + side, r), far_slot(2 * p_from + side, r),
            f2_send.at[p_to, r], f2_recv.at[p_from, r], (row, 2 * p_to + side),
        )

    def far3(r, p, s):
        return remote(
            far_slot(2 * p + s, r), far_slot(2 * p + s, r),
            f3_send.at[p, r], f3_recv.at[p, r], partner,
        )

    def mid_copy(c_to, c_from):
        span = mid_buf.at[pl.ds(pl.multiple_of(c_from * mids, mids), mids), :]
        return remote(span, span, mid_send.at[c_to], mid_recv.at[c_from], (row, c_to))

    def near_copy(slot, i, src, device):
        return remote(
            src, near.at[slot, i], near_send.at[slot, i], near_recv.at[slot, i], device
        )

    own = (k_ref, v_ref)
    ahead = at(lax.rem(pos + 2, total))

    def loop(low, high, f):
        def step(i, _):
            f(i)
            return 0

        lax.fori_loop(low, high, step, 0)

    loop(row + 1, rows, lambda r: far1(r, row).start())
    loop(col + 1, cols, lambda c: mid_copy(c, col).start())

    @pl.when(side == 0)
    def _():
        for i in range(2):
            near_copy(FROM_PARTNER, i, own[i], partner).start()

    @pl.when(pos + 2 < total)
    def _():
        for i in range(2):
            near_copy(FROM_BEHIND, i, own[i], ahead).start()

    def head_lanes(h, base=0):
        return pl.ds(pl.multiple_of(base + h * DH, DH), DH)

    def query_of(h):
        q = q_ref[:, pl.ds(pl.multiple_of(h * GROUP * DH, DH), GROUP * DH)]
        return jnp.concatenate([q[:, g * DH:(g + 1) * DH] for g in range(GROUP)], axis=0)

    def tiled_mask(seen, s):
        lines, keys = seen.shape
        shaped = s.reshape(GROUP, lines, keys)
        return shaped, seen[None]

    def masked(seen, s, fill):
        shaped, seen = tiled_mask(seen, s)
        return jnp.where(seen, shaped, fill).reshape(s.shape)

    def iota(shape, axis):
        return lax.broadcasted_iota(jnp.int32, shape, axis)

    def near_first(with_partner):
        def one(h):
            q = query_of(h)
            seen = iota((tok, tok), 1) <= iota((tok, tok), 0)
            s = masked(seen, score(q, k_ref[:, head_lanes(h)]), NEG_FILL)
            top = jnp.max(s, axis=-1, keepdims=True)
            if with_partner:
                s2 = score(q, near[FROM_PARTNER, 0, :, head_lanes(h)])
                top = jnp.maximum(top, jnp.max(s2, axis=-1, keepdims=True))
            acc = weigh(powers(s, top), v_ref[:, head_lanes(h)])
            if with_partner:
                acc = acc + weigh(powers(s2, top), near[FROM_PARTNER, 1, :, head_lanes(h)])
            acc_ref[h] = acc
            top_ref[h] = top

        loop(0, HK, one)

    @pl.when(side == 0)
    def _():
        near_first(False)

    def pass_on(r):
        far1(r, r).wait_recv()

        def to_pair(p):
            @pl.when(p != pair)
            def _():
                far2(r, p, pair).start()

        loop(0, pairs, to_pair)
        far3(r, pair, side).start()

    def far_pass():
        loop(0, row, pass_on)

    @pl.when(side == 0)
    def _():
        far_pass()

    @pl.when(side == 1)
    def _():
        for i in range(2):
            near_copy(FROM_PARTNER, i, own[i], partner).wait_recv()
        near_first(True)
        far_pass()

    loop(0, col, lambda c: mid_copy(c, c).wait_recv())
    n_mid = mid_buf.shape[0]

    def mid_one(h):
        q = query_of(h)
        seen = (iota((tok, n_mid), 1) * MID + MID - 1) <= (iota((tok, n_mid), 0) + col * tok)
        s = masked(seen, score(q, mid_buf[:, head_lanes(h)]), NEG_FILL)
        top = jnp.max(s, axis=-1, keepdims=True)
        p = masked(seen, powers(s, top), 0.0)
        rest_ref[h] = normalised(weigh(p, mid_buf[:, head_lanes(h, KV)]))

    loop(0, HK, mid_one)

    def pass_partner(r):
        def from_pair(p):
            @pl.when(p != pair)
            def _():
                far2(r, p, p).wait_recv()
                far3(r, p, side).start()

        loop(0, pairs, from_pair)

    loop(0, row, pass_partner)
    loop(0, row, lambda r: loop(0, pairs, lambda p: far3(r, p, 1 - side).wait_recv()))

    line = far_buf.shape[1]
    per = max(1, min(cols, FAR_CHUNK // line))
    n_chunk = cols // per

    def far_one(h):
        q = query_of(h)
        seen = lax.rem(iota((1, per * line), 1), line) < row * fars

        def part(j, base):
            block = far_buf[pl.ds(j * per, per), :, head_lanes(h, base)]
            return block.reshape(per * line, DH)

        def chunk(j, carry):
            s = jnp.where(seen, score(q, part(j, 0)), NEG_FILL)
            top = jnp.max(s, axis=-1, keepdims=True)
            if carry is None:
                return top, weigh(powers(s, top), part(j, KV))
            before, acc = carry
            top = jnp.maximum(before, top)
            return top, acc * powers(before, top) + weigh(powers(s, top), part(j, KV))

        carry = chunk(0, None)
        if n_chunk > 1:
            carry = lax.fori_loop(1, n_chunk, chunk, carry)
        rest_ref[h] = rest_ref[h] + normalised(carry[1])

    @pl.when(row > 0)
    def _():
        loop(0, HK, far_one)

    def put(h, value):
        for g in range(GROUP):
            lanes = pl.ds(pl.multiple_of((h * GROUP + g) * DH, DH), DH)
            out_ref[:, lanes] = value[g * tok:(g + 1) * tok].astype(out_ref.dtype)

    @pl.when(pos < 2)
    def _():
        loop(0, HK, lambda h: put(h, normalised(acc_ref[h]) + rest_ref[h]))

    @pl.when(pos >= 2)
    def _():
        for i in range(2):
            near_copy(FROM_BEHIND, i, own[i], ahead).wait_recv()
            near_copy(RELAYED, i, near.at[FROM_BEHIND, i], partner).start()
        for i in range(2):
            near_copy(RELAYED, i, near.at[FROM_BEHIND, i], partner).wait_recv()

        def one(h):
            q = query_of(h)
            before = top_ref[h]
            s1 = score(q, near[FROM_BEHIND, 0, :, head_lanes(h)])
            s2 = score(q, near[RELAYED, 0, :, head_lanes(h)])
            top = jnp.maximum(
                before,
                jnp.max(jnp.maximum(s1, s2), axis=-1, keepdims=True),
            )
            acc = acc_ref[h] * powers(before, top)
            acc = acc + weigh(powers(s1, top), near[FROM_BEHIND, 1, :, head_lanes(h)])
            acc = acc + weigh(powers(s2, top), near[RELAYED, 1, :, head_lanes(h)])
            put(h, normalised(acc) + rest_ref[h])

        loop(0, HK, one)

    loop(row + 1, rows, lambda r: far1(r, row).wait_send())
    loop(col + 1, cols, lambda c: mid_copy(c, col).wait_send())

    def sent(r):
        def one(p):
            far3(r, p, side).wait_send()

            @pl.when(p != pair)
            def _():
                far2(r, p, pair).wait_send()

        loop(0, pairs, one)

    loop(0, row, sent)

    @pl.when(side == 0)
    def _():
        for i in range(2):
            near_copy(FROM_PARTNER, i, own[i], partner).wait_send()

    @pl.when(pos + 2 < total)
    def _():
        for i in range(2):
            near_copy(FROM_BEHIND, i, own[i], ahead).wait_send()

    @pl.when(pos >= 2)
    def _():
        for i in range(2):
            near_copy(RELAYED, i, near.at[FROM_BEHIND, i], partner).wait_send()


def body(rows, cols, queries, keys, values, *weights):
    tok = queries.shape[0]
    assert BLOCK == 2 * tok and cols % 2 == 0
    dma = pltpu.SemaphoreType.DMA
    bf16, f32 = jnp.bfloat16, jnp.float32
    lines = GROUP * tok
    vmem = pl.BlockSpec(memory_space=pltpu.VMEM)
    return pl.pallas_call(
        functools.partial(kernel, rows, cols),
        out_shape=jax.ShapeDtypeStruct(queries.shape, bf16),
        in_specs=[vmem] * 7,
        out_specs=vmem,
        scratch_shapes=[
            pltpu.VMEM((2 * HK, tok, DH), f32),
            pltpu.VMEM((cols * (tok // MID), 2 * KV), bf16),
            pltpu.VMEM((tok // FAR, 2 * KV), bf16),
            pltpu.VMEM((cols, rows * (tok // FAR), 2 * KV), bf16),
            pltpu.VMEM((3, 2, tok, KV), bf16),
            pltpu.VMEM((HK, lines, 1), f32),
            pltpu.VMEM((HK, lines, 2 * DH), f32),
            pltpu.VMEM((HK, lines, DH), f32),
            dma((3, 2)),
            dma((3, 2)),
            dma((cols,)),
            dma((cols,)),
            dma((rows,)),
            dma((rows,)),
            dma((cols // 2, rows)),
            dma((cols // 2, rows)),
            dma((cols // 2, rows)),
            dma((cols // 2, rows)),
        ],
        compiler_params=pltpu.CompilerParams(
            collective_id=0, has_side_effects=True, vmem_limit_bytes=60 * 1024 * 1024
        ),
    )(queries, keys, values, *weights)


def solution(mesh):
    spec = P(("row", "col"), None)
    return jax.shard_map(
        functools.partial(body, mesh.shape["row"], mesh.shape["col"]),
        mesh=mesh,
        in_specs=(spec, spec, spec, P(), P(), P(), P()),
        out_specs=spec,
        check_vma=False,
    )
```

time: 126 us -> 47.2 us (0.37)
  the two profiles are of different devices: /device:TPU:0 before, /device:TPU:17 now
where the time goes in v1:
time: 47.2 us; the launch traced here: 47 us
  Pallas kernels  44.7 us (95%)
  local copies, waits for them, and re-layouts  2.3 us (5%)
    pallas_call x1, Pallas kernels, body(): pl.pallas_call(functools.partial(kernel, rows, cols), out_shape=jax.Shape...  44.7 us
    unnamed x1, local copies, waits for them, and re-layouts  2.3 us

profile of v1, /device:TPU:17, one launch (start us, length us, event | category | flops | bytes accessed | tf_op | source)
XLA Modules:
  0.0 47.0 jit_solution(16610963440976556537)
XLA Ops:
  0.0 44.7 %shard_map.73 = bf16[256,2048]{1,0:T(8,128)(2,1)} custom-call(bf16[256,2048]{1,0:T(8,128)(2,1)} %q_ref.1, bf16[256,512]{1,0:T(8,128)(2,1)} %k_ref.1, bf16[256,512]{1,0:T(8,128)(2,1)} %v_ref.1, bf16[1024,128]{1,0:T(8,128)(2,1)} %wmk_ref.1, bf16[1024,128]{1,0:T(8,128)(2,1)} %wmv_ref.1, bf16[2048,128]{1,0:T(8,128)(2,1)} %wfk_ref.1, bf16[2048,128]{1,0:T(8,128)(2,1)} %wfv_ref.1), custom_call_target="tpu_custom_call" | custom-call | tf_op jit(solution)/shard_map/pallas_call | solution.py:364
  44.7 2.3 %copy.9 = bf16[256,2048]{1,0:T(8,128)(2,1)} copy(bf16[256,2048]{1,0:T(8,128)(2,1)} %shard_map.73) | data formatting | bytes 2097152

commit v2 on v1

--- a/solution.py
+++ b/solution.py
@@ -19,6 +19,7 @@
 NEG_FILL = -1e30
 EXP_SCALE = DH ** (-0.5) * math.log2(math.e)
 FAR_CHUNK = 512
+VMEM_LIMIT = 60 * 1024 * 1024
 MESH = pl.DeviceIdType.MESH
 FROM_PARTNER, FROM_BEHIND, RELAYED = 0, 1, 2
 
@@ -42,7 +43,8 @@
 
 def kernel(
     rows, cols,
-    q_ref, k_ref, v_ref, wmk_ref, wmv_ref, wfk_ref, wfv_ref, out_ref,
+    q_hbm, k_hbm, v_hbm, wmk_hbm, wmv_hbm, wfk_hbm, wfv_hbm, out_ref,
+    q_ref, k_ref, v_ref, wmk_ref, wmv_ref, wfk_ref, wfv_ref, fetch_sem,
     wide, mid_buf, far_own, far_buf, near, top_ref, acc_ref, rest_ref,
     near_send, near_recv, mid_send, mid_recv,
     f1_send, f1_recv, f2_send, f2_recv, f3_send, f3_recv,
@@ -58,6 +60,19 @@
     other = col + 1 - 2 * side
     partner = (row, other)
 
+    def fetch(i, src, dst):
+        return pltpu.make_async_copy(src, dst, fetch_sem.at[i])
+
+    fetches = [
+        fetch(i, src, dst)
+        for i, (src, dst) in enumerate((
+            (k_hbm, k_ref), (wfk_hbm, wfk_ref), (wmk_hbm, wmk_ref),
+            (v_hbm, v_ref), (wfv_hbm, wfv_ref), (wmv_hbm, wmv_ref), (q_hbm, q_ref),
+        ))
+    ]
+    for copy in fetches:
+        copy.start()
+
     def at(linear):
         return (linear // cols, lax.rem(linear, cols))
 
@@ -87,8 +102,76 @@
     greet(at(lax.rem(pos + 2, total)))
     greet(at(lax.rem(pos + total - 2, total)))
 
+
+    def head_lanes(h, base=0):
+        return pl.ds(pl.multiple_of(base + h * DH, DH), DH)
+
+    def remote(src, dst, send, recv, device):
+        return pltpu.make_async_remote_copy(
+            src_ref=src, dst_ref=dst, send_sem=send, recv_sem=recv,
+            device_id=device, device_id_type=MESH,
+        )
+
+    def far_slot(c, r):
+        return far_buf.at[c, pl.ds(pl.multiple_of(r * fars, fars), fars), :]
+
+    def far1(r_to, r_from):
+        return remote(far_own, far_slot(col, r_from), f1_send.at[r_to], f1_recv.at[r_from], (r_to, col))
+
+    def far2(r, p_to, p_from):
+        return remote(
+            far_slot(2 * p_from + side, r), far_slot(2 * p_from + side, r),
+            f2_send.at[p_to, r], f2_recv.at[p_from, r], (row, 2 * p_to + side),
+        )
+
+    def far3(r, p, s):
+        return remote(
+            far_slot(2 * p + s, r), far_slot(2 * p + s, r),
+            f3_send.at[p, r], f3_recv.at[p, r], partner,
+        )
+
+    def mid_copy(c_to, c_from):
+        span = mid_buf.at[pl.ds(pl.multiple_of(c_from * mids, mids), mids), :]
+        return remote(span, span, mid_send.at[c_to], mid_recv.at[c_from], (row, c_to))
+
+    def near_copy(slot, i, src, device):
+        return remote(
+            src, near.at[slot, i], near_send.at[slot, i, 0], near_recv.at[slot, i, 0], device
+        )
+
+    def behind_copy(i, h):
+        lanes = head_lanes(h)
+        return remote(
+            own[i].at[:, lanes], near.at[FROM_BEHIND, i, :, lanes],
+            near_send.at[FROM_BEHIND, i, h], near_recv.at[FROM_BEHIND, i, h], ahead,
+        )
+
+    def relay_copy(i, h):
+        lanes = head_lanes(h)
+        return remote(
+            near.at[FROM_BEHIND, i, :, lanes], near.at[RELAYED, i, :, lanes],
+            near_send.at[RELAYED, i, h], near_recv.at[RELAYED, i, h], partner,
+        )
+
+    def behind_start(h):
+        for i in range(2):
+            behind_copy(i, h).start()
+
+    own = (k_ref, v_ref)
+    ahead = at(lax.rem(pos + 2, total))
+
+    def loop(low, high, f):
+        def step(i, _):
+            f(i)
+            return 0
+
+        lax.fori_loop(low, high, step, 0)
+
     mid_rows = pl.ds(pl.multiple_of(col * mids, mids), mids)
-    for s, (src, wm, wf) in enumerate(((k_ref, wmk_ref, wfk_ref), (v_ref, wmv_ref, wfv_ref))):
+
+    def summarise(s, src, wm, wf):
+        for copy in fetches[4 * s:3 * s + 3]:
+            copy.wait()
         for h in range(HK):
             wide[s * HK + h] = src[:, h * DH:(h + 1) * DH].astype(jnp.float32)
         for squeeze, count, weight in ((FAR, fars, wf), (MID, mids, wm)):
@@ -112,50 +195,15 @@
                 else:
                     mid_buf[mid_rows, lanes] = piece
 
+    summarise(0, k_ref, wmk_ref, wfk_ref)
+    fetches[3].wait()
     pl.semaphore_wait(barrier, cols + rows)
 
-    def remote(src, dst, send, recv, device):
-        return pltpu.make_async_remote_copy(
-            src_ref=src, dst_ref=dst, send_sem=send, recv_sem=recv,
-            device_id=device, device_id_type=MESH,
-        )
-
-    def far_slot(c, r):
-        return far_buf.at[c, pl.ds(pl.multiple_of(r * fars, fars), fars), :]
-
-    def far1(r_to, r_from):
-        return remote(far_own, far_slot(col, r_from), f1_send.at[r_to], f1_recv.at[r_from], (r_to, col))
-
-    def far2(r, p_to, p_from):
-        return remote(
-            far_slot(2 * p_from + side, r), far_slot(2 * p_from + side, r),
-            f2_send.at[p_to, r], f2_recv.at[p_from, r], (row, 2 * p_to + side),
-        )
-
-    def far3(r, p, s):
-        return remote(
-            far_slot(2 * p + s, r), far_slot(2 * p + s, r),
-            f3_send.at[p, r], f3_recv.at[p, r], partner,
-        )
-
-    def mid_copy(c_to, c_from):
-        span = mid_buf.at[pl.ds(pl.multiple_of(c_from * mids, mids), mids), :]
-        return remote(span, span, mid_send.at[c_to], mid_recv.at[c_from], (row, c_to))
-
-    def near_copy(slot, i, src, device):
-        return remote(
-            src, near.at[slot, i], near_send.at[slot, i], near_recv.at[slot, i], device
-        )
-
-    own = (k_ref, v_ref)
-    ahead = at(lax.rem(pos + 2, total))
-
-    def loop(low, high, f):
-        def step(i, _):
-            f(i)
-            return 0
-
-        lax.fori_loop(low, high, step, 0)
+    @pl.when(pos + 2 < total)
+    def _():
+        behind_start(0)
+
+    summarise(1, v_ref, wmv_ref, wfv_ref)
 
     loop(row + 1, rows, lambda r: far1(r, row).start())
     loop(col + 1, cols, lambda c: mid_copy(c, col).start())
@@ -167,15 +215,19 @@
 
     @pl.when(pos + 2 < total)
     def _():
-        for i in range(2):
-            near_copy(FROM_BEHIND, i, own[i], ahead).start()
-
-    def head_lanes(h, base=0):
-        return pl.ds(pl.multiple_of(base + h * DH, DH), DH)
+        loop(1, HK, behind_start)
+
+    fetches[6].wait()
 
     def query_of(h):
         q = q_ref[:, pl.ds(pl.multiple_of(h * GROUP * DH, DH), GROUP * DH)]
         return jnp.concatenate([q[:, g * DH:(g + 1) * DH] for g in range(GROUP)], axis=0)
+
+    def queries_of(h):
+        base = h * GROUP * DH
+        return [
+            q_ref[:, pl.ds(pl.multiple_of(base + g * DH, DH), DH)] for g in range(GROUP)
+        ]
 
     def tiled_mask(seen, s):
         lines, keys = seen.shape
@@ -191,18 +243,20 @@
 
     def near_first(with_partner):
         def one(h):
-            q = query_of(h)
             seen = iota((tok, tok), 1) <= iota((tok, tok), 0)
-            s = masked(seen, score(q, k_ref[:, head_lanes(h)]), NEG_FILL)
-            top = jnp.max(s, axis=-1, keepdims=True)
+            key_parts = [k_ref[:, head_lanes(h)]]
+            value_parts = [v_ref[:, head_lanes(h)]]
             if with_partner:
-                s2 = score(q, near[FROM_PARTNER, 0, :, head_lanes(h)])
-                top = jnp.maximum(top, jnp.max(s2, axis=-1, keepdims=True))
-            acc = weigh(powers(s, top), v_ref[:, head_lanes(h)])
-            if with_partner:
-                acc = acc + weigh(powers(s2, top), near[FROM_PARTNER, 1, :, head_lanes(h)])
-            acc_ref[h] = acc
-            top_ref[h] = top
+                key_parts.append(near[FROM_PARTNER, 0, :, head_lanes(h)])
+                value_parts.append(near[FROM_PARTNER, 1, :, head_lanes(h)])
+            s = [[score(q, k) for k in key_parts] for q in queries_of(h)]
+            for g, parts in enumerate(s):
+                parts = [jnp.where(seen, parts[0], NEG_FILL)] + parts[1:]
+                top = jnp.max(functools.reduce(jnp.maximum, parts), axis=-1, keepdims=True)
+                span = slice(g * tok, (g + 1) * tok)
+                terms = [weigh(powers(p, top), v) for p, v in zip(parts, value_parts)]
+                acc_ref[h, span] = functools.reduce(jnp.add, terms)
+                top_ref[h, span] = top
 
         loop(0, HK, one)
 
@@ -246,7 +300,7 @@
         p = masked(seen, powers(s, top), 0.0)
         rest_ref[h] = normalised(weigh(p, mid_buf[:, head_lanes(h, KV)]))
 
-    loop(0, HK, mid_one)
+    loop(0, HK // 2, mid_one)
 
     def pass_partner(r):
         def from_pair(p):
@@ -258,6 +312,7 @@
         loop(0, pairs, from_pair)
 
     loop(0, row, pass_partner)
+    loop(HK // 2, HK, mid_one)
     loop(0, row, lambda r: loop(0, pairs, lambda p: far3(r, p, 1 - side).wait_recv()))
 
     line = far_buf.shape[1]
@@ -286,40 +341,65 @@
             carry = lax.fori_loop(1, n_chunk, chunk, carry)
         rest_ref[h] = rest_ref[h] + normalised(carry[1])
 
-    @pl.when(row > 0)
-    def _():
-        loop(0, HK, far_one)
-
-    def put(h, value):
-        for g in range(GROUP):
-            lanes = pl.ds(pl.multiple_of((h * GROUP + g) * DH, DH), DH)
-            out_ref[:, lanes] = value[g * tok:(g + 1) * tok].astype(out_ref.dtype)
+    def put(h, g, value):
+        lanes = pl.ds(pl.multiple_of((h * GROUP + g) * DH, DH), DH)
+        out_ref[:, lanes] = value.astype(out_ref.dtype)
+
+    def arrive(h):
+        for i in range(2):
+            behind_copy(i, h).wait_recv()
+            relay_copy(i, h).start()
+
+    def near_last(h):
+        for i in range(2):
+            relay_copy(i, h).wait_recv()
+        parts = (FROM_BEHIND, RELAYED)
+        s = [
+            [score(q, near[slot, 0, :, head_lanes(h)]) for slot in parts]
+            for q in queries_of(h)
+        ]
+        for g, pair_s in enumerate(s):
+            span = slice(g * tok, (g + 1) * tok)
+            before = top_ref[h, span]
+            top = jnp.maximum(before, jnp.max(jnp.maximum(*pair_s), axis=-1, keepdims=True))
+            acc = acc_ref[h, span] * powers(before, top)
+            for slot, part in zip(parts, pair_s):
+                acc = acc + weigh(powers(part, top), near[slot, 1, :, head_lanes(h)])
+            put(h, g, normalised(acc) + rest_ref[h, span])
+
+    def far_step(h):
+        @pl.when(row > 0)
+        def _():
+            far_one(h)
+
+    lead = HK // 2
+    loop(0, lead, far_step)
+
+    @pl.when(pos >= 2)
+    def _():
+        arrive(0)
+
+    def step(h):
+        @pl.when(h + lead < HK)
+        def _():
+            far_step(h + lead)
+
+        @pl.when((pos >= 2) & (h + 1 < HK))
+        def _():
+            arrive(h + 1)
+
+        @pl.when(pos >= 2)
+        def _():
+            near_last(h)
+
+    loop(0, HK, step)
 
     @pl.when(pos < 2)
     def _():
-        loop(0, HK, lambda h: put(h, normalised(acc_ref[h]) + rest_ref[h]))
-
-    @pl.when(pos >= 2)
-    def _():
-        for i in range(2):
-            near_copy(FROM_BEHIND, i, own[i], ahead).wait_recv()
-            near_copy(RELAYED, i, near.at[FROM_BEHIND, i], partner).start()
-        for i in range(2):
-            near_copy(RELAYED, i, near.at[FROM_BEHIND, i], partner).wait_recv()
-
         def one(h):
-            q = query_of(h)
-            before = top_ref[h]
-            s1 = score(q, near[FROM_BEHIND, 0, :, head_lanes(h)])
-            s2 = score(q, near[RELAYED, 0, :, head_lanes(h)])
-            top = jnp.maximum(
-                before,
-                jnp.max(jnp.maximum(s1, s2), axis=-1, keepdims=True),
-            )
-            acc = acc_ref[h] * powers(before, top)
-            acc = acc + weigh(powers(s1, top), near[FROM_BEHIND, 1, :, head_lanes(h)])
-            acc = acc + weigh(powers(s2, top), near[RELAYED, 1, :, head_lanes(h)])
-            put(h, normalised(acc) + rest_ref[h])
+            for g in range(GROUP):
+                span = slice(g * tok, (g + 1) * tok)
+                put(h, g, normalised(acc_ref[h, span]) + rest_ref[h, span])
 
         loop(0, HK, one)
 
@@ -346,12 +426,12 @@
     @pl.when(pos + 2 < total)
     def _():
         for i in range(2):
-            near_copy(FROM_BEHIND, i, own[i], ahead).wait_send()
+            loop(0, HK, lambda h, i=i: behind_copy(i, h).wait_send())
 
     @pl.when(pos >= 2)
     def _():
         for i in range(2):
-            near_copy(RELAYED, i, near.at[FROM_BEHIND, i], partner).wait_send()
+            loop(0, HK, lambda h, i=i: relay_copy(i, h).wait_send())
 
 
 def body(rows, cols, queries, keys, values, *weights):
@@ -364,9 +444,11 @@
     return pl.pallas_call(
         functools.partial(kernel, rows, cols),
         out_shape=jax.ShapeDtypeStruct(queries.shape, bf16),
-        in_specs=[vmem] * 7,
+        in_specs=[pl.BlockSpec(memory_space=pltpu.HBM)] * 7,
         out_specs=vmem,
         scratch_shapes=[
+            *[pltpu.VMEM(a.shape, a.dtype) for a in (queries, keys, values, *weights)],
+            dma((7,)),
             pltpu.VMEM((2 * HK, tok, DH), f32),
             pltpu.VMEM((cols * (tok // MID), 2 * KV), bf16),
             pltpu.VMEM((tok // FAR, 2 * KV), bf16),
@@ -375,8 +457,8 @@
             pltpu.VMEM((HK, lines, 1), f32),
             pltpu.VMEM((HK, lines, 2 * DH), f32),
             pltpu.VMEM((HK, lines, DH), f32),
-            dma((3, 2)),
-            dma((3, 2)),
+            dma((3, 2, HK)),
+            dma((3, 2, HK)),
             dma((cols,)),
             dma((cols,)),
             dma((rows,)),
@@ -387,7 +469,7 @@
             dma((cols // 2, rows)),
         ],
         compiler_params=pltpu.CompilerParams(
-            collective_id=0, has_side_effects=True, vmem_limit_bytes=60 * 1024 * 1024
+            collective_id=0, has_side_effects=True, vmem_limit_bytes=VMEM_LIMIT
         ),
     )(queries, keys, values, *weights)
 

time: 47.2 us -> 41.7 us (0.88)
  Pallas kernels: 44.7 us -> 39.2 us
    pallas_call x1, Pallas kernels: 44.7 us -> 39.2 us  [body(): pl.pallas_call(functools.partial(kernel, rows, cols), out_shape=jax.Shape...]
where the time goes in v2:
time: 41.7 us; the launch traced here: 41.5 us
  Pallas kernels  39.2 us (94%)
  local copies, waits for them, and re-layouts  2.3 us (6%)
    pallas_call x1, Pallas kernels, body(): pl.pallas_call(functools.partial(kernel, rows, cols), out_shape=jax.Shape...  39.2 us
    unnamed x1, local copies, waits for them, and re-layouts  2.3 us

profile of v2, /device:TPU:17, one launch (start us, length us, event | category | flops | bytes accessed | tf_op | source)
XLA Modules:
  0.0 41.5 jit_solution(4446606911360612533)
XLA Ops:
  0.0 39.2 %shard_map.73 = bf16[256,2048]{1,0:T(8,128)(2,1)} custom-call(bf16[256,2048]{1,0:T(8,128)(2,1)} %q_hbm.1, bf16[256,512]{1,0:T(8,128)(2,1)} %k_hbm.1, bf16[256,512]{1,0:T(8,128)(2,1)} %v_hbm.1, bf16[1024,128]{1,0:T(8,128)(2,1)} %wmk_hbm.1, bf16[1024,128]{1,0:T(8,128)(2,1)} %wmv_hbm.1, bf16[2048,128]{1,0:T(8,128)(2,1)} %wfk_hbm.1, bf16[2048,128]{1,0:T(8,128)(2,1)} %wfv_hbm.1), custom_call_target="tpu_custom_call" | custom-call | tf_op jit(solution)/shard_map/pallas_call | solution.py:444
  39.2 2.3 %copy.9 = bf16[256,2048]{1,0:T(8,128)(2,1)} copy(bf16[256,2048]{1,0:T(8,128)(2,1)} %shard_map.73) | data formatting | bytes 2097152

commit v3 on v2

--- a/solution.py
+++ b/solution.py
@@ -19,7 +19,7 @@
 NEG_FILL = -1e30
 EXP_SCALE = DH ** (-0.5) * math.log2(math.e)
 FAR_CHUNK = 512
-VMEM_LIMIT = 60 * 1024 * 1024
+VMEM_LIMIT = 57 * 1024 * 1024
 MESH = pl.DeviceIdType.MESH
 FROM_PARTNER, FROM_BEHIND, RELAYED = 0, 1, 2
 
@@ -443,7 +443,7 @@
     vmem = pl.BlockSpec(memory_space=pltpu.VMEM)
     return pl.pallas_call(
         functools.partial(kernel, rows, cols),
-        out_shape=jax.ShapeDtypeStruct(queries.shape, bf16),
+        out_shape=pltpu.VMEM(queries.shape, bf16),
         in_specs=[pl.BlockSpec(memory_space=pltpu.HBM)] * 7,
         out_specs=vmem,
         scratch_shapes=[

time: 41.7 us -> 39.3 us (0.942)
  local copies, waits for them, and re-layouts: 2.3 us -> 0.97 us
  Pallas kernels: 39.2 us -> 38.2 us
    unnamed x1, local copies, waits for them, and re-layouts: 2.3 us -> 0.97 us
    pallas_call x1, Pallas kernels: 39.2 us -> 38.2 us  [body(): pl.pallas_call(functools.partial(kernel, rows, cols), out_shape=pltpu.VME...]
where the time goes in v3:
time: 39.3 us; the launch traced here: 39.2 us
  Pallas kernels  38.2 us (97%)
  local copies, waits for them, and re-layouts  0.97 us (2%)
    pallas_call x1, Pallas kernels, body(): pl.pallas_call(functools.partial(kernel, rows, cols), out_shape=pltpu.VME...  38.2 us
    unnamed x1, local copies, waits for them, and re-layouts  0.97 us

profile of v3, /device:TPU:17, one launch (start us, length us, event | category | flops | bytes accessed | tf_op | source)
XLA Modules:
  0.0 39.2 jit_solution(18261889131966550100)
XLA Ops:
  0.0 38.2 %shard_map.73 = bf16[256,2048]{1,0:T(8,128)(2,1)S(1)} custom-call(bf16[256,2048]{1,0:T(8,128)(2,1)} %q_hbm.1, bf16[256,512]{1,0:T(8,128)(2,1)} %k_hbm.1, bf16[256,512]{1,0:T(8,128)(2,1)} %v_hbm.1, bf16[1024,128]{1,0:T(8,128)(2,1)} %wmk_hbm.1, bf16[1024,128]{1,0:T(8,128)(2,1)} %wmv_hbm.1, bf16[2048,128]{1,0:T(8,128)(2,1)} %wfk_hbm.1, bf16[2048,128]{1,0:T(8,128)(2,1)} %wfv_hbm.1), custom_call_target="tpu_custom_call" | custom-call | tf_op jit(solution)/shard_map/pallas_call | solution.py:444
  38.2 1.0 %copy.9 = bf16[256,2048]{1,0:T(8,128)(2,1)} copy(bf16[256,2048]{1,0:T(8,128)(2,1)S(1)} %shard_map.73) | data formatting | bytes 2097152
